TPU v7x, 8 devices: a whole 2x2x1 slice. The times are simulated.
8 devices in a mesh: data: 1 (over z), pp: 2 (over y), ep: 4 (over x, core).
Axes of the slice: x: 2, y: 2, z: 1, core: 2. Of those that a mesh axis runs over, the one named last changes fastest.
Arguments:
- o: bfloat16 [2, 1, 384, 32, 7168], P('pp', 'data', 'ep')
- idx: int32 [2, 1, 4, 256, 8], P('pp', 'data')
- slot: int32 [2, 1, 4, 256, 8], P('pp', 'data')
- gate: float32 [2, 1, 4, 256, 8], P('pp', 'data')
- h: bfloat16 [2, 1, 4, 256, 7168], P('pp', 'data', 'ep')
- norm_w: float32 [2, 7168], P('pp')
- wq: bfloat16 [2, 7168, 8192], P('pp')
- wk: bfloat16 [2, 7168, 8192], P('pp')
- wv: bfloat16 [2, 7168, 8192], P('pp')
- wo: bfloat16 [2, 8192, 7168], P('pp')
Outputs:
- output: bfloat16 [2, 1, 4, 256, 7168], P('pp', 'data', 'ep')
All inputs are finite; a program needn't handle non-finite values.
Results may differ from a plain program's by a relative error of at most 0.0106752.
Values are sent between devices in bfloat16 or wider.
A program may use at most 2 GiB of HBM per device.

v0:
```python
import jax
import jax.numpy as jnp
from jax import lax
from jax.sharding import PartitionSpec as P

HEAD = 128
EPS = 1e-6
SCALE = HEAD ** -0.5


def attend(y, nw, wq, wk, wv, wo):
    nm, ns, ln, d = y.shape
    hd = wq.shape[1]
    nh = hd // HEAD
    yf = y.astype(jnp.float32)
    x = yf * lax.rsqrt(jnp.mean(yf * yf, axis=-1, keepdims=True) + EPS) * nw
    xb = x.astype(jnp.bfloat16)
    shp = (nm, ns, ln, nh, HEAD)
    q = jnp.einsum('msld,de->msle', xb, wq, preferred_element_type=jnp.float32).astype(jnp.bfloat16).reshape(shp)
    kt = jnp.einsum('msld,de->msle', xb, wk, preferred_element_type=jnp.float32).astype(jnp.bfloat16).reshape(shp)
    vt = jnp.einsum('msld,de->msle', xb, wv, preferred_element_type=jnp.float32).astype(jnp.bfloat16).reshape(shp)
    sc = jnp.einsum('msqhd,mskhd->mshqk', q, kt, preferred_element_type=jnp.float32) * SCALE
    causal = lax.broadcasted_iota(jnp.int32, (ln, ln), 0) >= lax.broadcasted_iota(jnp.int32, (ln, ln), 1)
    pr = jax.nn.softmax(jnp.where(causal, sc, -1e30), axis=-1).astype(jnp.bfloat16)
    att = jnp.einsum('mshqk,mskhd->msqhd', pr, vt, preferred_element_type=jnp.float32).astype(jnp.bfloat16).reshape(nm, ns, ln, hd)
    out = jnp.einsum('msle,ed->msld', att, wo, preferred_element_type=jnp.float32).astype(jnp.bfloat16)
    return (yf + out.astype(jnp.float32)).astype(jnp.bfloat16)


def gsum(table, flat, gw):
    fi = jnp.moveaxis(flat, -1, 0)
    rows = table[fi].astype(jnp.float32)
    return jnp.sum(jnp.moveaxis(gw, -1, 0)[..., None] * rows, axis=0)


def solution(mesh):
    n = mesh.shape['ep']
    npp = mesh.shape['pp']
    perm = [(i, (i + 1) % npp) for i in range(npp)]
    sp_o = P('pp', 'data', 'ep', None, None)
    sp_r = P('pp', 'data', None, None, None)
    sp_1 = P('pp', None)
    sp_w = P('pp', None, None)

    def body(o, idx, slot, gate, h, norm_w, wq, wk, wv, wo):
        o = o[0]
        nm, el, c, d = o.shape
        capd = c // n
        ns, ln, kk = h.shape[2], h.shape[3], idx.shape[4]
        me = lax.axis_index('ep')
        xs = jnp.moveaxis(o.reshape(nm, el, n, capd, d), 2, 0)
        recv = lax.all_to_all(xs, 'ep', 0, 0, tiled=True)
        table = recv.reshape(n * nm * el * capd, d)
        ix = lax.dynamic_slice_in_dim(idx[0], me * ns, ns, axis=1)
        sl = lax.dynamic_slice_in_dim(slot[0], me * ns, ns, axis=1)
        gg = lax.dynamic_slice_in_dim(gate[0], me * ns, ns, axis=1)
        valid = sl >= 0
        mo = lax.broadcasted_iota(jnp.int32, ix.shape, 0)
        flat = jnp.where(valid, (((ix // el) * nm + mo) * el + ix % el) * capd + sl - me * capd, 0)
        gw = jnp.where(valid, gg, 0.0)
        y = (h[0].astype(jnp.float32) + gsum(table, flat, gw)).astype(jnp.bfloat16)
        yin = lax.ppermute(y, 'pp', perm)
        z = attend(yin, norm_w[0], wq[0], wk[0], wv[0], wo[0])
        return z[None]

    return jax.shard_map(body, mesh=mesh, in_specs=(sp_o, sp_r, sp_r, sp_r, sp_o, sp_1, sp_w, sp_w, sp_w, sp_w), out_specs=sp_o, check_vma=False)
```

profile of v0, /device:TPU:0, one launch (start us, length us, event | category | flops | bytes accessed | tf_op | source)
XLA Modules:
  0.0 1022.3 jit_solution(13953669211642584778)
XLA Ops:
  0.0 29.7 %copy.20 = bf16[4,1,96,8,7168]{4,3,2,1,0:T(8,128)(2,1)} copy(bf16[4,1,96,8,7168]{4,3,0,2,1:T(8,128)(2,1)} %bitcast.133) | data formatting | bytes 88080384 | tf_op jit(solution)/shard_map/transpose | solution.py:51
  29.7 0.0 copy-start.3
  29.7 11.6 %all-to-all-start = ((bf16[4,1,96,8,7168]{4,3,2,1,0:T(8,128)(2,1)}), bf16[4,1,96,8,7168]{4,3,2,1,0:T(8,128)(2,1)}, u32[]{:S(2)}, u32[]{:S(2)}) async-start(bf16[4,1,96,8,7168]{4,3,2,1,0:T(8,128)(2,1)} %copy.20), calls=%async_computation | async-start | bytes 88080384 | tf_op jit(solution)/shard_map/all_to_all | solution.py:52
  41.3 0.0 copy-done.3
  41.3 0.7 fusion.65
  42.0 0.7 fusion.66
  42.7 474.4 %all-to-all-done = bf16[4,1,96,8,7168]{4,3,2,1,0:T(8,128)(2,1)} async-done(((bf16[4,1,96,8,7168]{4,3,2,1,0:T(8,128)(2,1)}), bf16[4,1,96,8,7168]{4,3,2,1,0:T(8,128)(2,1)}, u32[]{:S(2)}, u32[]{:S(2)}) %all-to-all-start) | async-done | bytes 44040224 | tf_op jit(solution)/shard_map/all_to_all | solution.py:52
  517.1 171.6 %gather_fusion = bf16[2048,7168]{1,0:T(8,128)(2,1)} fusion(bf16[3072,7168]{1,0:T(8,128)(2,1)} %bitcast.7, s32[2048]{0:T(1024)S(1)} %broadcast_clamp_fusion), kind=kCustom, calls=%fused_computation | custom fusion | bytes 58728448 | tf_op jit(solution)/shard_map/gather | solution.py:32
  688.7 13.7 %fusion.9 = f32[256,7168]{1,0:T(8,128)} fusion(bf16[8,1,1,256,7168]{4,3,0,2,1:T(8,128)(2,1)} %bitcast.132, f32[8,256]{1,0:T(8,128)S(1)} %fusion.66), kind=kLoop, calls=%fused_computation.11 | loop fusion | flops 42205184 | bytes 36708352 | tf_op jit(solution)/shard_map/reduce_sum | solution.py:33
  702.5 0.0 copy-start.4
  702.5 5.1 fusion.44
  707.5 3.9 collective-permute-start
  711.5 0.7 iota_compare_fusion
  712.1 78.2 %collective-permute-done = bf16[1,1,256,7168]{3,2,1,0:T(8,128)(2,1)S(1)} collective-permute-done((bf16[1,1,256,7168]{3,2,1,0:T(8,128)(2,1)S(1)}, bf16[1,1,256,7168]{3,2,1,0:T(8,128)(2,1)S(1)}, u32[]{:S(2)}, u32[]{:S(2)}) %collective-permute-start) | collective-permute-done | bytes 3670048 | tf_op jit(solution)/shard_map/ppermute | solution.py:62
  790.4 0.0 copy-start
  790.4 1.8 copy-done
  792.2 0.8 fusion.41
  793.0 0.0 copy-done.4
  793.0 46.6 %fusion.11 = bf16[256,8192]{1,0:T(8,128)(2,1)} fusion(bf16[1,7168,8192]{2,1,0:T(8,128)(2,1)} %param.18, bf16[1,1,256,7168]{3,2,1,0:T(8,128)(2,1)} %copy-done, f32[7168]{0:T(1024)S(1)} %bitcast.137, f32[256]{0:T(256)S(1)} %add_rsqrt_fusion), kind=kOutput, calls=%fused_computation.19 | convolution fusion | flops 30074208256 | bytes 125334528 | tf_op jit(solution)/shard_map/msld,de->msle/dot_general | solution.py:21
  839.6 6.4 copy.26
  846.0 46.7 %fusion.52 = bf16[32,64,8,128]{3,2,1,0:T(8,128)(2,1)} fusion(bf16[1,7168,8192]{2,1,0:T(8,128)(2,1)} %param.17, bf16[1,1,256,7168]{3,2,1,0:T(8,128)(2,1)} %copy-done, f32[7168]{0:T(1024)S(1)} %bitcast.138, f32[256]{0:T(256)S(1)} %add_rsqrt_fusion), kind=kOutput, calls=%fused_computation.43 | convolution fusion | flops 30074208256 | bytes 125334528 | tf_op jit(solution)/shard_map/msld,de->msle/dot_general | solution.py:20
  892.7 46.5 %fusion.55 = bf16[32,64,8,128]{3,2,1,0:T(8,128)(2,1)} fusion(bf16[1,7168,8192]{2,1,0:T(8,128)(2,1)} %param.16, bf16[1,1,256,7168]{3,2,1,0:T(8,128)(2,1)} %copy-done, f32[7168]{0:T(1024)S(1)} %bitcast.139, f32[256]{0:T(256)S(1)} %add_rsqrt_fusion), kind=kOutput, calls=%fused_computation.44 | convolution fusion | flops 30074208256 | bytes 125334528 | tf_op jit(solution)/shard_map/msld,de->msle/dot_general | solution.py:19
  939.2 0.0 copy-start.2
  939.2 11.6 %fusion.45 = f32[64,256,256]{1,2,0:T(8,128)} fusion(bf16[32,64,8,128]{3,2,1,0:T(8,128)(2,1)} %fusion.52, bf16[32,64,8,128]{3,2,1,0:T(8,128)(2,1)} %fusion.55), kind=kOutput, calls=%fused_computation.36 | convolution fusion | flops 1073741824 | bytes 25165824 | tf_op jit(solution)/shard_map/msqhd,mskhd->mshqk/dot_general | solution.py:22
  950.8 0.0 copy-done.2
  950.8 18.0 %fusion.75 = (f32[64,256]{1,0:T(8,128)S(1)}, f32[64,256,256]{1,2,0:T(8,128)}) fusion(f32[64,256,256]{1,2,0:T(8,128)} %fusion.45, pred[256,256]{0,1:T(8,128)(4,1)S(1)} %copy-done.2), kind=kOutput, calls=%fused_computation.70 | output fusion | flops 25166080 | bytes 33685504 | tf_op jit(solution)/shard_map/sub | solution.py:24
  968.8 0.0 copy-start.1
  968.8 8.7 fusion.51
  977.5 0.0 copy-done.1
  977.5 44.9 %fusion.34 = bf16[1,1,1,256,7168]{4,3,2,1,0:T(8,128)(2,1)} fusion(bf16[256,8192]{0,1:T(8,128)(2,1)S(1)} %bitcast.134, bf16[1,8192,7168]{2,1,0:T(8,128)(2,1)} %param.19, bf16[1,1,256,7168]{3,2,1,0:T(8,128)(2,1)S(1)} %copy-done.1), kind=kOutput, calls=%fused_computation.26 | convolution fusion | flops 30073946112 | bytes 128974848 | tf_op jit(solution)/shard_map/msle,ed->msld/dot_general | solution.py:26
  (3 shorter events, 0.0 us)
Async XLA Ops:
  29.7 11.6 %copy-start.3 = (s32[1,1,4,256,8]{3,4,2,1,0:T(8,128)S(1)}, s32[1,1,4,256,8]{3,4,2,1,0:T(8,128)}, u32[]{:S(2)}) copy-start(s32[1,1,4,256,8]{3,4,2,1,0:T(8,128)} %param.12) | copy-start | bytes 98308
  29.7 487.4 %all-to-all-start = ((bf16[4,1,96,8,7168]{4,3,2,1,0:T(8,128)(2,1)}), bf16[4,1,96,8,7168]{4,3,2,1,0:T(8,128)(2,1)}, u32[]{:S(2)}, u32[]{:S(2)}) async-start(bf16[4,1,96,8,7168]{4,3,2,1,0:T(8,128)(2,1)} %copy.20), calls=%async_computation | async-start | bytes 88080384 | tf_op jit(solution)/shard_map/all_to_all | solution.py:52
  702.5 90.6 %copy-start.4 = (f32[1,7168]{1,0:T(1,128)S(1)}, f32[1,7168]{1,0:T(1,128)}, u32[]{:S(2)}) copy-start(f32[1,7168]{1,0:T(1,128)} %param.15) | copy-start | bytes 86020
  707.5 82.8 %collective-permute-start = (bf16[1,1,256,7168]{3,2,1,0:T(8,128)(2,1)S(1)}, bf16[1,1,256,7168]{3,2,1,0:T(8,128)(2,1)S(1)}, u32[]{:S(2)}, u32[]{:S(2)}) collective-permute-start(bf16[1,1,256,7168]{3,2,1,0:T(8,128)(2,1)S(1)} %fusion.44), channel_id=1, source_target_pairs={{0,4},{4,0},{1,5},{5,1},{2,6},{6,2},{3,7},{7,3}} | collective-permute-start | bytes 11010056 | tf_op jit(solution)/shard_map/ppermute | solution.py:62
  790.4 1.8 copy-start
  939.2 11.6 %copy-start.2 = (pred[256,256]{0,1:T(8,128)(4,1)S(1)}, pred[256,256]{0,1:T(8,128)(4,1)}, u32[]{:S(2)}) copy-start(pred[256,256]{0,1:T(8,128)(4,1)} %iota_compare_fusion) | copy-start | bytes 196612
  968.8 8.7 copy-start.1
where the time goes:
time: 1020 us
  waiting for transfers between devices  553 us (54%)
  local copies, waits for them, and re-layouts  210 us (21%)
  matrix products  205 us (20%)
  other arithmetic  39.7 us (4%)
  starting transfers between devices  15.5 us (2%)
    all_to_all x1, waiting for transfers between devices, body(): recv = lax.all_to_all(xs, 'ep', 0, 0, tiled=True)  474 us
    gather x1, local copies, waits for them, and re-layouts, gsum(): rows = table[fi].astype(jnp.float32)  172 us
    ppermute x1, waiting for transfers between devices, body(): yin = lax.ppermute(y, 'pp', perm)  78.2 us
    dot_general x1, matrix products, attend(): jnp.einsum('msld,de->msle', xb, wk, preferred_element_type=jnp.float32)  46.7 us
    dot_general x1, matrix products, attend(): jnp.einsum('msld,de->msle', xb, wv, preferred_element_type=jnp.float32)  46.6 us
    dot_general x1, matrix products, attend(): jnp.einsum('msld,de->msle', xb, wq, preferred_element_type=jnp.float32)  46.5 us
    dot_general x1, matrix products, attend(): jnp.einsum('msle,ed->msld', att, wo, preferred_element_type=jnp.float32)  44.9 us
    transpose x1, local copies, waits for them, and re-layouts, body(): xs = jnp.moveaxis(o.reshape(nm, el, n, capd, d), 2, 0)  29.7 us
  transfers between devices with their start and end apart: 2, of which 2 were waited for; matrix products, arithmetic and copies ran while one was open for 0% of the time, Pallas kernels for 0%

commit v1 on v0

v1 whole, which is shorter than its diff:
```python
import functools

import jax
import jax.numpy as jnp
from jax import lax
from jax.experimental import pallas as pl
from jax.experimental.pallas import tpu as pltpu
from jax.sharding import PartitionSpec as P

HEAD = 128
EPS = 1e-6
SCALE = HEAD ** -0.5
MESH = pl.DeviceIdType.MESH
F32 = jnp.float32
BF16 = jnp.bfloat16
CH = 512
NS = 4
WN = 2048
SHIFT = 2.0 ** -40


def kernel(n_ep, el, capd, idx_ref, slot_ref, gate_ref, nw_ref, o_hbm, h_hbm, wq_hbm, wk_hbm, wv_hbm, wo_hbm,
           z_hbm, send, base, xrecv, yin, ssq, rs_ref,
           s_d2r, r_d2r, s_d2o, r_d2o, s_x, r_x, s_y, r_y, s_w, s_o, s_h, s_z):
    p = lax.axis_index('pp')
    me = lax.axis_index('ep')
    mate = me + 1 - 2 * lax.rem(me, 2)
    xpeer = lax.rem(me + 2, n_ep)
    xmate = mate + 2 - 4 * (mate // 2)
    ydev = {'pp': 1 - p}
    xdev = {'ep': xpeer}
    mdev = {'ep': mate}
    nc = send.shape[0]
    ln = send.shape[1]
    ns = el * capd
    nh = wq_hbm.shape[1] // HEAD
    ng = nh * HEAD // CH
    d = wo_hbm.shape[1]
    wj = wq_hbm.shape[1] // WN
    hbms = (wq_hbm, wk_hbm, wv_hbm)

    barrier = pltpu.get_barrier_semaphore()
    for dev in (mdev, xdev, ydev):
        pl.semaphore_signal(barrier, inc=1, device_id=dev, device_id_type=MESH)
    pl.semaphore_wait(barrier, 3)

    dests = (xmate, mate, xpeer, me)

    def produce(gm, oslab, stage, hbuf):
        def ocopy(n, q):
            sl = lax.rem(n, 2)
            return pltpu.make_async_copy(
                o_hbm.at[:, dests[q], :, pl.ds(pl.multiple_of(n * CH, CH), CH)], oslab.at[sl, q], s_o.at[sl, q])

        hcopy = pltpu.make_async_copy(h_hbm, hbuf, s_h)
        hcopy.start()
        for q in range(4):
            ocopy(0, q).start()
        iota = lax.broadcasted_iota(jnp.int32, (ln, ns), 1)

        def build(q):
            j = dests[q]
            loc = idx_ref[j] - el * me
            sl = slot_ref[j]
            ok = (sl >= 0) & (loc >= 0) & (loc < el)
            flat = jnp.where(ok, loc * capd + sl - j * capd, -1)
            gt = gate_ref[j]
            a = jnp.zeros((ln, ns), F32)
            for k in range(flat.shape[1]):
                a = a + jnp.where(iota == flat[:, k:k + 1], gt[:, k:k + 1], 0.0)
            g1 = a.astype(BF16)
            a = a - g1.astype(F32)
            g2 = a.astype(BF16)
            a = a - g2.astype(F32)
            gm[q, 0:ln] = g1
            gm[q, ln:2 * ln] = g2
            gm[q, 2 * ln:3 * ln] = a.astype(BF16)

        for q in range(4):
            build(q)
        hcopy.wait()

        def rsend(n):
            return pltpu.make_async_remote_copy(stage.at[0, lax.rem(n, 2)], send.at[n], s_d2r.at[lax.rem(n, 2)], r_d2r.at[n],
                                                device_id=mdev, device_id_type=MESH)

        def osend(n):
            return pltpu.make_async_remote_copy(stage.at[1, lax.rem(n, 2)], base.at[n], s_d2o.at[lax.rem(n, 2)], r_d2o.at[n],
                                                device_id=mdev, device_id_type=MESH)

        def part(n, q):
            ocopy(n, q).wait()
            r = jnp.dot(gm[q], oslab[lax.rem(n, 2), q].reshape(ns, CH), preferred_element_type=F32)
            return r[0:ln] + r[ln:2 * ln] + r[2 * ln:3 * ln]

        def step(n, _):
            @pl.when(n + 1 < nc)
            def _():
                for q in range(4):
                    ocopy(n + 1, q).start()

            @pl.when(n >= 2)
            def _():
                rsend(n - 2).wait_send()
                osend(n - 2).wait_send()
            b = lax.rem(n, 2)
            stage[0, b] = part(n, 0)
            rsend(n).start()
            stage[1, b] = part(n, 1)
            osend(n).start()
            mine = part(n, 2)
            rsend(n).wait_recv()
            send[n] = send[n] + mine
            own = part(n, 3) + hbuf[:, pl.ds(pl.multiple_of(n * CH, CH), CH)].astype(F32)
            xsend(n).start()
            osend(n).wait_recv()
            base[n] = base[n] + own
            return 0

        lax.fori_loop(0, nc, step, 0)
        for n in (nc - 2, nc - 1):
            rsend(n).wait_send()
            osend(n).wait_send()

    def xsend(n):
        return pltpu.make_async_remote_copy(send.at[n], xrecv.at[n], s_x.at[n], r_x.at[n],
                                            device_id=xdev, device_id_type=MESH)

    pl.run_scoped(produce,
                  pltpu.VMEM((4, 3 * ln, ns), BF16),
                  pltpu.VMEM((2, 4, el, capd, CH), BF16),
                  pltpu.VMEM((2, 2, ln, CH), F32),
                  pltpu.VMEM((ln, d), BF16))

    def main(acc, wbuf, ystage):
        def wcopy(n, i):
            src = hbms[i // wj].at[pl.ds(pl.multiple_of(n * CH, CH), CH), pl.ds((i % wj) * WN, WN)]
            return pltpu.make_async_copy(src, wbuf.at[i % NS], s_w.at[i % NS])

        def ocopy(g, i):
            wd = min(WN, d - i * WN)
            src = wo_hbm.at[pl.ds(pl.multiple_of(g * CH, CH), CH), pl.ds(i * WN, wd)]
            return pltpu.make_async_copy(src, wbuf.at[i, :, 0:wd], s_w.at[i])

        def ysend(n):
            return pltpu.make_async_remote_copy(ystage.at[lax.rem(n, 2)], yin.at[n], s_y.at[lax.rem(n, 2)], r_y.at[n],
                                                device_id=ydev, device_id_type=MESH)

        for i in range(NS):
            wcopy(0, i).start()

        def zero(i, _):
            acc[i] = jnp.zeros(acc.shape[1:], F32)
            return 0
        lax.fori_loop(0, acc.shape[0], zero, 0)
        ssq[...] = jnp.zeros_like(ssq)

        def service(n):
            @pl.when(n >= 2)
            def _():
                ysend(n - 2).wait_send()
            xsend(n).wait_recv()
            ystage[lax.rem(n, 2)] = (base[n] + xrecv[n]).astype(BF16)
            ysend(n).start()

        service(0)
        nj = 3 * wj

        def chunk(n, _):
            @pl.when(n + 1 < nc)
            def _():
                service(n + 1)
            ysend(n).wait_recv()
            yf = yin[n].astype(F32)
            y2 = yf * yf
            ssq[...] += y2[:, 0:128] + y2[:, 128:256] + y2[:, 256:384] + y2[:, 384:512]
            xw = (yf * (nw_ref[n] * SHIFT)).astype(BF16)
            for i in range(nj):
                wcopy(n, i).wait()
                for b in range(WN // CH):
                    k = i * (WN // CH) + b
                    acc[k] += jnp.dot(xw, wbuf[i % NS, :, b * CH:(b + 1) * CH], preferred_element_type=F32)
                if i + NS < nj:
                    wcopy(n, i + NS).start()
                else:
                    ii = i + NS - nj

                    @pl.when(n + 1 < nc)
                    def _():
                        wcopy(n + 1, ii).start()

                    @pl.when(n + 1 == nc)
                    def _():
                        ocopy(0, ii).start()
            return 0

        lax.fori_loop(0, nc, chunk, 0)
        ysend(nc - 2).wait_send()
        ysend(nc - 1).wait_send()
        for n in range(nc):
            xsend(n).wait_send()

        def zero2(i, _):
            send[i] = jnp.zeros(send.shape[1:], F32)
            return 0
        lax.fori_loop(0, nc, zero2, 0)
        ms = jnp.sum(ssq[...], axis=1, keepdims=True) / d
        rs_ref[...] = jnp.broadcast_to(lax.rsqrt(ms + EPS) * (1.0 / SHIFT), rs_ref.shape)

        row = lax.broadcasted_iota(jnp.int32, (ln, ln), 0)
        col = lax.broadcasted_iota(jnp.int32, (ln, ln), 1)

        def group(g, _):
            rs = rs_ref[:, 0:1]
            q4 = (acc[g] * rs).astype(BF16)
            k4 = (acc[ng + g] * rs).astype(BF16)
            v4 = (acc[2 * ng + g] * rs).astype(BF16)
            outs = []
            for hh in range(CH // HEAD):
                c = slice(hh * HEAD, (hh + 1) * HEAD)
                s = lax.dot_general(q4[:, c], k4[:, c], (((1,), (1,)), ((), ())), preferred_element_type=F32) * SCALE
                s = jnp.where(row >= col, s, -1e30)
                e = jnp.exp(s - jnp.max(s, axis=1, keepdims=True))
                pr = (e * (1.0 / jnp.sum(e, axis=1, keepdims=True))).astype(BF16)
                outs.append(jnp.dot(pr, v4[:, c], preferred_element_type=F32).astype(BF16))
            a4 = jnp.concatenate(outs, axis=1)
            for i in range(NS):
                ocopy(g, i).wait()
                wd = min(WN, d - i * WN)
                for b in range(wd // CH):
                    k = i * (WN // CH) + b
                    send[k] += jnp.dot(a4, wbuf[i, :, b * CH:(b + 1) * CH], preferred_element_type=F32)

                @pl.when(g + 1 < ng)
                def _():
                    ocopy(g + 1, i).start()
            return 0

        lax.fori_loop(0, ng, group, 0)

        def zcopy(n):
            return pltpu.make_async_copy(yin.at[n], z_hbm.at[:, pl.ds(pl.multiple_of(n * CH, CH), CH)], s_z.at[n])

        def fin(n, _):
            yin[n] = (yin[n].astype(F32) + send[n].astype(BF16).astype(F32)).astype(BF16)
            zcopy(n).start()
            return 0
        lax.fori_loop(0, nc, fin, 0)

        def finw(n, _):
            zcopy(n).wait()
            return 0
        lax.fori_loop(0, nc, finw, 0)

    pl.run_scoped(main,
                  pltpu.VMEM((3 * ng, ln, CH), F32),
                  pltpu.VMEM((NS, CH, WN), BF16),
                  pltpu.VMEM((2, ln, CH), BF16))


def solution(mesh):
    n = mesh.shape['ep']
    sp_o = P('pp', 'data', 'ep', None, None)
    sp_r = P('pp', 'data', None, None, None)
    sp_1 = P('pp', None)
    sp_w = P('pp', None, None)

    def body(o, idx, slot, gate, h, norm_w, wq, wk, wv, wo):
        el, c, d = o.shape[2:]
        capd = c // n
        ln = h.shape[3]
        nc = d // CH
        ng = wq.shape[2] // CH
        sem = pltpu.SemaphoreType.DMA
        vm = pl.BlockSpec(memory_space=pltpu.VMEM)
        hb = pl.BlockSpec(memory_space=pltpu.HBM)
        z = pl.pallas_call(
            functools.partial(kernel, n, el, capd),
            out_shape=jax.ShapeDtypeStruct((ln, d), BF16),
            in_specs=[vm] * 4 + [hb] * 6,
            out_specs=hb,
            scratch_shapes=[
                pltpu.VMEM((nc, ln, CH), F32),
                pltpu.VMEM((nc, ln, CH), F32),
                pltpu.VMEM((nc, ln, CH), F32),
                pltpu.VMEM((nc, ln, CH), BF16),
                pltpu.VMEM((ln, 128), F32),
                pltpu.VMEM((ln, 128), F32),
                sem((2,)), sem((nc,)), sem((2,)), sem((nc,)), sem((nc,)), sem((nc,)), sem((2,)), sem((nc,)),
                sem((NS,)), sem((2, 4)), sem, sem((nc,)),
            ],
            compiler_params=pltpu.CompilerParams(collective_id=0, has_side_effects=True, vmem_limit_bytes=67043328),
        )(idx[0, 0], slot[0, 0], gate[0, 0], norm_w.reshape(nc, 1, CH), o.reshape(el, n, capd, d), h[0, 0, 0],
          wq[0], wk[0], wv[0], wo[0])
        return z.reshape(1, 1, 1, ln, d)

    return jax.shard_map(body, mesh=mesh, in_specs=(sp_o, sp_r, sp_r, sp_r, sp_o, sp_1, sp_w, sp_w, sp_w, sp_w), out_specs=sp_o, check_vma=False)
```

time: 1020 us -> 265 us (0.26)
  waiting for transfers between devices: 553 us -> 0 us
  Pallas kernels: 0 us -> 256 us
  matrix products: 205 us -> 0 us
  local copies, waits for them, and re-layouts: 210 us -> 9.4 us
  other arithmetic: 39.7 us -> 0 us
  starting transfers between devices: 15.5 us -> 0 us
    all_to_all x1 -> x0, waiting for transfers between devices: 474 us -> none  [body(): recv = lax.all_to_all(xs, 'ep', 0, 0, tiled=True)]
    pallas_call x0 -> x1, Pallas kernels: none -> 256 us  [body(): pl.pallas_call(functools.partial(kernel, n, el, capd), out_shape=jax.Shap...]
    dot_general x6 -> x0, matrix products: 205 us -> none  [the longest x1 46.7 us: attend(): jnp.einsum('msld,de->msle', xb, wk, preferred_element_type=jnp.float32)]
    gather x1 -> x0, local copies, waits for them, and re-layouts: 172 us -> none  [gsum(): rows = table[fi].astype(jnp.float32)]
    ppermute x1 -> x0, waiting for transfers between devices: 78.2 us -> none  [body(): yin = lax.ppermute(y, 'pp', perm)]
    transpose x1 -> x0, local copies, waits for them, and re-layouts: 29.7 us -> none  [body(): xs = jnp.moveaxis(o.reshape(nm, el, n, capd, d), 2, 0)]
    sub x1 -> x0, other arithmetic: 18 us -> none  [attend(): jax.nn.softmax(jnp.where(causal, sc, -1e+30), axis=-1).astype(jnp.bfloat16)]
    reduce_sum x2 -> x0, other arithmetic: 14.5 us -> none  [the longest x1 13.7 us: gsum(): return jnp.sum(jnp.moveaxis(gw, -1, 0)[..., None] * rows, axis=0)]
  transfers between devices with their start and end apart: 2 -> 0, of which waited for: 2 -> 0; matrix products, arithmetic and copies ran while one was open for 0% -> 0% of each run, Pallas kernels for 0% -> 0%
where the time goes in v1:
time: 265 us
  Pallas kernels  256 us (97%)
  local copies, waits for them, and re-layouts  9.4 us (4%)
    pallas_call x1, Pallas kernels, body(): pl.pallas_call(functools.partial(kernel, n, el, capd), out_shape=jax.Shap...  256 us
    unnamed x4, local copies, waits for them, and re-layouts  9.4 us

profile of v1, /device:TPU:0, one launch (start us, length us, event | category | flops | bytes accessed | tf_op | source)
XLA Modules:
  0.0 265.0 jit_solution(12930732687987073865)
XLA Ops:
  0.0 1.8 copy.11
  1.8 1.8 copy.12
  3.5 1.8 copy.13
  5.3 255.6 %shard_map.100 = bf16[256,7168]{1,0:T(8,128)(2,1)} custom-call(s32[4,256,8]{2,1,0:T(8,128)} %bitcast.14, s32[4,256,8]{2,1,0:T(8,128)} %bitcast.15, f32[4,256,8]{2,1,0:T(8,128)} %bitcast.16, f32[14,1,512]{2,1,0:T(1,128)} %bitcast.17, bf16[96,4,8,7168]{3,2,1,0:T(8,128)(2,1)} %bitcast.11, bf16[256,7168]{1,0:T(8,128)(2,1)} %bitcast.13, ...), custom_call_target="tpu_custom_call" | custom-call | tf_op jit(solution)/shard_map/pallas_call | solution.py:277
  260.9 4.1 %copy.15 = bf16[1,1,1,256,7168]{4,3,2,1,0:T(8,128)(2,1)} copy(bf16[1,1,1,256,7168]{4,3,2,1,0:T(8,128)(2,1)} %bitcast.12) | data formatting | bytes 7340032

commit v2 on v1

--- a/solution.py
+++ b/solution.py
@@ -10,6 +10,9 @@
 HEAD = 128
 EPS = 1e-6
 SCALE = HEAD ** -0.5
+SCALE2 = SCALE * 1.4426950408889634
+MASKED = -1e30 / SCALE
+QB = 128
 MESH = pl.DeviceIdType.MESH
 F32 = jnp.float32
 BF16 = jnp.bfloat16
@@ -17,11 +20,12 @@
 NS = 4
 WN = 2048
 SHIFT = 2.0 ** -40
+HEADS_AT = ((0, 1, 2, 3), (), (), ())
 
 
 def kernel(n_ep, el, capd, idx_ref, slot_ref, gate_ref, nw_ref, o_hbm, h_hbm, wq_hbm, wk_hbm, wv_hbm, wo_hbm,
            z_hbm, send, base, xrecv, yin, ssq, rs_ref,
-           s_d2r, r_d2r, s_d2o, r_d2o, s_x, r_x, s_y, r_y, s_w, s_o, s_h, s_z):
+           s_d2r, r_d2r, s_d2o, r_d2o, s_x, r_x, s_y, r_y, s_w, s_o, s_h):
     p = lax.axis_index('pp')
     me = lax.axis_index('ep')
     mate = me + 1 - 2 * lax.rem(me, 2)
@@ -42,7 +46,6 @@
     barrier = pltpu.get_barrier_semaphore()
     for dev in (mdev, xdev, ydev):
         pl.semaphore_signal(barrier, inc=1, device_id=dev, device_id_type=MESH)
-    pl.semaphore_wait(barrier, 3)
 
     dests = (xmate, mate, xpeer, me)
 
@@ -63,10 +66,13 @@
             loc = idx_ref[j] - el * me
             sl = slot_ref[j]
             ok = (sl >= 0) & (loc >= 0) & (loc < el)
-            flat = jnp.where(ok, loc * capd + sl - j * capd, -1)
-            gt = gate_ref[j]
+            kk = sl.shape[0]
+            pad = jnp.zeros((128 - kk, ln), F32)
+            flat = jnp.where(ok, loc * capd + sl - j * capd, -1).astype(F32)
+            flat = jnp.concatenate([flat, pad], axis=0).T[:, 0:kk].astype(jnp.int32)
+            gt = jnp.concatenate([gate_ref[j], pad], axis=0).T[:, 0:kk]
             a = jnp.zeros((ln, ns), F32)
-            for k in range(flat.shape[1]):
+            for k in range(kk):
                 a = a + jnp.where(iota == flat[:, k:k + 1], gt[:, k:k + 1], 0.0)
             g1 = a.astype(BF16)
             a = a - g1.astype(F32)
@@ -76,9 +82,6 @@
             gm[q, ln:2 * ln] = g2
             gm[q, 2 * ln:3 * ln] = a.astype(BF16)
 
-        for q in range(4):
-            build(q)
-        hcopy.wait()
 
         def rsend(n):
             return pltpu.make_async_remote_copy(stage.at[0, lax.rem(n, 2)], send.at[n], s_d2r.at[lax.rem(n, 2)], r_d2r.at[n],
@@ -93,31 +96,60 @@
             r = jnp.dot(gm[q], oslab[lax.rem(n, 2), q].reshape(ns, CH), preferred_element_type=F32)
             return r[0:ln] + r[ln:2 * ln] + r[2 * ln:3 * ln]
 
-        def step(n, _):
+        def fetch(n):
             @pl.when(n + 1 < nc)
             def _():
                 for q in range(4):
                     ocopy(n + 1, q).start()
 
-            @pl.when(n >= 2)
-            def _():
-                rsend(n - 2).wait_send()
-                osend(n - 2).wait_send()
-            b = lax.rem(n, 2)
-            stage[0, b] = part(n, 0)
+        def away(n):
+            stage[0, lax.rem(n, 2)] = part(n, 0)
             rsend(n).start()
-            stage[1, b] = part(n, 1)
-            osend(n).start()
+
+        def away2(n):
             mine = part(n, 2)
             rsend(n).wait_recv()
             send[n] = send[n] + mine
+
+        def near(n):
+            stage[1, lax.rem(n, 2)] = part(n, 1)
+            osend(n).start()
+
+        def near2(n):
+            own = part(n, 3) + hbuf[:, pl.ds(pl.multiple_of(n * CH, CH), CH)].astype(F32)
+            osend(n).wait_recv()
+            base[n] = base[n] + own
+
+        fetch(0)
+        build(0)
+        pl.semaphore_wait(barrier, 3)
+        away(0)
+        build(2)
+        away2(0)
+        xsend(0).start()
+        build(1)
+        near(0)
+        build(3)
+        hcopy.wait()
+        near2(0)
+
+        def step(n, _):
+            fetch(n)
+
+            @pl.when(n >= 2)
+            def _():
+                rsend(n - 2).wait_send()
+                osend(n - 2).wait_send()
+            away(n)
+            near(n)
+            away2(n)
             own = part(n, 3) + hbuf[:, pl.ds(pl.multiple_of(n * CH, CH), CH)].astype(F32)
             xsend(n).start()
             osend(n).wait_recv()
             base[n] = base[n] + own
             return 0
 
-        lax.fori_loop(0, nc, step, 0)
+        lax.fori_loop(1, nc, step, 0)
         for n in (nc - 2, nc - 1):
             rsend(n).wait_send()
             osend(n).wait_send()
@@ -132,7 +164,7 @@
                   pltpu.VMEM((2, 2, ln, CH), F32),
                   pltpu.VMEM((ln, d), BF16))
 
-    def main(acc, wbuf, ystage):
+    def main(acc, wbuf, ystage, abuf0, abuf1):
         def wcopy(n, i):
             src = hbms[i // wj].at[pl.ds(pl.multiple_of(n * CH, CH), CH), pl.ds((i % wj) * WN, WN)]
             return pltpu.make_async_copy(src, wbuf.at[i % NS], s_w.at[i % NS])
@@ -163,6 +195,10 @@
             ystage[lax.rem(n, 2)] = (base[n] + xrecv[n]).astype(BF16)
             ysend(n).start()
 
+        def clear(n):
+            xsend(n).wait_send()
+            send[n] = jnp.zeros(send.shape[1:], F32)
+
         service(0)
         nj = 3 * wj
 
@@ -170,6 +206,9 @@
             @pl.when(n + 1 < nc)
             def _():
                 service(n + 1)
+            @pl.when(n >= 2)
+            def _():
+                clear(n - 2)
             ysend(n).wait_recv()
             yf = yin[n].astype(F32)
             y2 = yf * yf
@@ -197,65 +236,72 @@
         lax.fori_loop(0, nc, chunk, 0)
         ysend(nc - 2).wait_send()
         ysend(nc - 1).wait_send()
-        for n in range(nc):
-            xsend(n).wait_send()
-
-        def zero2(i, _):
-            send[i] = jnp.zeros(send.shape[1:], F32)
-            return 0
-        lax.fori_loop(0, nc, zero2, 0)
+        for n in (nc - 2, nc - 1):
+            clear(n)
         ms = jnp.sum(ssq[...], axis=1, keepdims=True) / d
         rs_ref[...] = jnp.broadcast_to(lax.rsqrt(ms + EPS) * (1.0 / SHIFT), rs_ref.shape)
 
-        row = lax.broadcasted_iota(jnp.int32, (ln, ln), 0)
-        col = lax.broadcasted_iota(jnp.int32, (ln, ln), 1)
-
-        def group(g, _):
+        tri = lax.broadcasted_iota(jnp.int32, (QB, QB), 0) >= lax.broadcasted_iota(jnp.int32, (QB, QB), 1)
+
+        def qkv(g, hh):
             rs = rs_ref[:, 0:1]
-            q4 = (acc[g] * rs).astype(BF16)
-            k4 = (acc[ng + g] * rs).astype(BF16)
-            v4 = (acc[2 * ng + g] * rs).astype(BF16)
-            outs = []
-            for hh in range(CH // HEAD):
-                c = slice(hh * HEAD, (hh + 1) * HEAD)
-                s = lax.dot_general(q4[:, c], k4[:, c], (((1,), (1,)), ((), ())), preferred_element_type=F32) * SCALE
-                s = jnp.where(row >= col, s, -1e30)
-                e = jnp.exp(s - jnp.max(s, axis=1, keepdims=True))
-                pr = (e * (1.0 / jnp.sum(e, axis=1, keepdims=True))).astype(BF16)
-                outs.append(jnp.dot(pr, v4[:, c], preferred_element_type=F32).astype(BF16))
-            a4 = jnp.concatenate(outs, axis=1)
+            c = slice(hh * HEAD, (hh + 1) * HEAD)
+            return [(acc[m * ng + g, :, c] * rs).astype(BF16) for m in range(3)]
+
+        def heads(g, hhs, dst):
+            tiles = [(hh, r) for hh in hhs for r in range(ln // QB)]
+            qk = {hh: qkv(g, hh) for hh in hhs}
+            sc = []
+            for hh, r in tiles:
+                lo, hi = r * QB, (r + 1) * QB
+                q, k, _ = qk[hh]
+                s = lax.dot_general(q[lo:hi], k[0:hi], (((1,), (1,)), ((), ())), preferred_element_type=F32)
+                t = jnp.where(tri, s[:, lo:hi], MASKED)
+                sc.append(t if r == 0 else jnp.concatenate([s[:, 0:lo], t], axis=1))
+            mx = [jnp.max(s, axis=1, keepdims=True) for s in sc]
+            ex = [jnp.exp2((s - m) * SCALE2) for s, m in zip(sc, mx)]
+            rc = [1.0 / jnp.sum(e, axis=1, keepdims=True) for e in ex]
+            pr = [(e * c).astype(BF16) for e, c in zip(ex, rc)]
+            for (hh, r), w in zip(tiles, pr):
+                lo, hi = r * QB, (r + 1) * QB
+                dst[lo:hi, hh * HEAD:(hh + 1) * HEAD] = jnp.dot(w, qk[hh][2][0:hi], preferred_element_type=F32).astype(BF16)
+
+        heads(0, range(CH // HEAD), abuf0)
+
+        def group(g, src, dst):
+            g1 = jnp.minimum(g + 1, ng - 1)
             for i in range(NS):
                 ocopy(g, i).wait()
                 wd = min(WN, d - i * WN)
                 for b in range(wd // CH):
                     k = i * (WN // CH) + b
-                    send[k] += jnp.dot(a4, wbuf[i, :, b * CH:(b + 1) * CH], preferred_element_type=F32)
+                    send[k] += jnp.dot(src[...], wbuf[i, :, b * CH:(b + 1) * CH], preferred_element_type=F32)
+                if HEADS_AT[i]:
+                    heads(g1, HEADS_AT[i], dst)
 
                 @pl.when(g + 1 < ng)
                 def _():
                     ocopy(g + 1, i).start()
-            return 0
-
-        lax.fori_loop(0, ng, group, 0)
-
-        def zcopy(n):
-            return pltpu.make_async_copy(yin.at[n], z_hbm.at[:, pl.ds(pl.multiple_of(n * CH, CH), CH)], s_z.at[n])
+
+        def pair(gg, _):
+            group(2 * gg, abuf0, abuf1)
+            group(2 * gg + 1, abuf1, abuf0)
+            return 0
+
+        lax.fori_loop(0, ng // 2, pair, 0)
 
         def fin(n, _):
-            yin[n] = (yin[n].astype(F32) + send[n].astype(BF16).astype(F32)).astype(BF16)
-            zcopy(n).start()
+            z_hbm[:, pl.ds(pl.multiple_of(n * CH, CH), CH)] = (
+                yin[n].astype(F32) + send[n].astype(BF16).astype(F32)).astype(BF16)
             return 0
         lax.fori_loop(0, nc, fin, 0)
-
-        def finw(n, _):
-            zcopy(n).wait()
-            return 0
-        lax.fori_loop(0, nc, finw, 0)
 
     pl.run_scoped(main,
                   pltpu.VMEM((3 * ng, ln, CH), F32),
                   pltpu.VMEM((NS, CH, WN), BF16),
-                  pltpu.VMEM((2, ln, CH), BF16))
+                  pltpu.VMEM((2, ln, CH), BF16),
+                  pltpu.VMEM((ln, CH), BF16),
+                  pltpu.VMEM((ln, CH), BF16))
 
 
 def solution(mesh):
@@ -276,9 +322,9 @@
         hb = pl.BlockSpec(memory_space=pltpu.HBM)
         z = pl.pallas_call(
             functools.partial(kernel, n, el, capd),
-            out_shape=jax.ShapeDtypeStruct((ln, d), BF16),
+            out_shape=pltpu.VMEM((ln, d), BF16),
             in_specs=[vm] * 4 + [hb] * 6,
-            out_specs=hb,
+            out_specs=vm,
             scratch_shapes=[
                 pltpu.VMEM((nc, ln, CH), F32),
                 pltpu.VMEM((nc, ln, CH), F32),
@@ -287,10 +333,10 @@
                 pltpu.VMEM((ln, 128), F32),
                 pltpu.VMEM((ln, 128), F32),
                 sem((2,)), sem((nc,)), sem((2,)), sem((nc,)), sem((nc,)), sem((nc,)), sem((2,)), sem((nc,)),
-                sem((NS,)), sem((2, 4)), sem, sem((nc,)),
+                sem((NS,)), sem((2, 4)), sem,
             ],
-            compiler_params=pltpu.CompilerParams(collective_id=0, has_side_effects=True, vmem_limit_bytes=67043328),
-        )(idx[0, 0], slot[0, 0], gate[0, 0], norm_w.reshape(nc, 1, CH), o.reshape(el, n, capd, d), h[0, 0, 0],
+            compiler_params=pltpu.CompilerParams(collective_id=0, has_side_effects=True, vmem_limit_bytes=63000000),
+        )(jnp.swapaxes(idx[0, 0], 1, 2), jnp.swapaxes(slot[0, 0], 1, 2), jnp.swapaxes(gate[0, 0], 1, 2), norm_w.reshape(nc, 1, CH), o.reshape(el, n, capd, d), h[0, 0, 0],
           wq[0], wk[0], wv[0], wo[0])
         return z.reshape(1, 1, 1, ln, d)
 

time: 265 us -> 242 us (0.913)
  Pallas kernels: 256 us -> 240 us
  local copies, waits for them, and re-layouts: 9.4 us -> 1.84 us
    pallas_call x1, Pallas kernels: 256 us -> 240 us  [body(): pl.pallas_call(functools.partial(kernel, n, el, capd), out_shape=pltpu.VM...]
    unnamed x4 -> x1, local copies, waits for them, and re-layouts: 9.4 us -> 1.84 us
where the time goes in v2:
time: 242 us
  Pallas kernels  240 us (99%)
    pallas_call x1, Pallas kernels, body(): pl.pallas_call(functools.partial(kernel, n, el, capd), out_shape=pltpu.VM...  240 us

profile of v2, /device:TPU:0, one launch (start us, length us, event | category | flops | bytes accessed | tf_op | source)
XLA Modules:
  0.0 242.0 jit_solution(4228733105631894959)
XLA Ops:
  0.0 240.1 %shard_map.100 = bf16[256,7168]{1,0:T(8,128)(2,1)S(1)} custom-call(s32[4,8,256]{2,1,0:T(8,128)} %bitcast.20, s32[4,8,256]{2,1,0:T(8,128)} %bitcast.21, f32[4,8,256]{2,1,0:T(8,128)} %bitcast.22, f32[14,1,512]{2,1,0:T(1,128)} %bitcast.23, bf16[96,4,8,7168]{3,2,1,0:T(8,128)(2,1)} %bitcast.18, bf16[256,7168]{1,0:T(8,128)(2,1)} %bitcast.19, ...), custom_call_target="tpu_custom_call" | custom-call | tf_op jit(solution)/shard_map/pallas_call | solution.py:323
  240.1 1.8 copy.12

commit v3 on v2

--- a/solution.py
+++ b/solution.py
@@ -20,11 +20,13 @@
 NS = 4
 WN = 2048
 SHIFT = 2.0 ** -40
+EARLY = (6, 10)
+LATE = 5
 HEADS_AT = ((0, 1, 2, 3), (), (), ())
 
 
 def kernel(n_ep, el, capd, idx_ref, slot_ref, gate_ref, nw_ref, o_hbm, h_hbm, wq_hbm, wk_hbm, wv_hbm, wo_hbm,
-           z_hbm, send, base, xrecv, yin, ssq, rs_ref,
+           z_hbm, send, base, xrecv, yin, ssq, rs_ref, ystage,
            s_d2r, r_d2r, s_d2o, r_d2o, s_x, r_x, s_y, r_y, s_w, s_o, s_h):
     p = lax.axis_index('pp')
     me = lax.axis_index('ep')
@@ -48,6 +50,43 @@
         pl.semaphore_signal(barrier, inc=1, device_id=dev, device_id_type=MESH)
 
     dests = (xmate, mate, xpeer, me)
+
+    def xsend(n):
+        return pltpu.make_async_remote_copy(send.at[n], xrecv.at[n], s_x.at[n], r_x.at[n],
+                                            device_id=xdev, device_id_type=MESH)
+
+    def ysend(n):
+        return pltpu.make_async_remote_copy(ystage.at[lax.rem(n, 2)], yin.at[n], s_y.at[lax.rem(n, 2)], r_y.at[n],
+                                            device_id=ydev, device_id_type=MESH)
+
+    hr = ln // 2
+
+    def xlast(f):
+        c = pl.ds(f * hr, hr)
+        return pltpu.make_async_remote_copy(send.at[nc - 1, c], xrecv.at[nc - 1, c], s_x.at[nc - 1 + f], r_x.at[nc - 1 + f],
+                                            device_id=xdev, device_id_type=MESH)
+
+    def ylast(f):
+        c = pl.ds(f * hr, hr)
+        b = (nc - 1) % 2
+        return pltpu.make_async_remote_copy(ystage.at[b, c], yin.at[nc - 1, c], s_y.at[b + f], r_y.at[nc - 1 + f],
+                                            device_id=ydev, device_id_type=MESH)
+
+    def service_last(f):
+        if f == 0:
+            ysend(nc - 3).wait_send()
+        xlast(f).wait_recv()
+        c = slice(f * hr, (f + 1) * hr)
+        ystage[(nc - 1) % 2, c] = (base[nc - 1, c] + xrecv[nc - 1, c]).astype(BF16)
+        ylast(f).start()
+
+    def service(n):
+        @pl.when(n >= 2)
+        def _():
+            ysend(n - 2).wait_send()
+        xsend(n).wait_recv()
+        ystage[lax.rem(n, 2)] = (base[n] + xrecv[n]).astype(BF16)
+        ysend(n).start()
 
     def produce(gm, oslab, stage, hbuf):
         def ocopy(n, q):
@@ -144,19 +183,26 @@
             near(n)
             away2(n)
             own = part(n, 3) + hbuf[:, pl.ds(pl.multiple_of(n * CH, CH), CH)].astype(F32)
-            xsend(n).start()
+            @pl.when(n < nc - 1)
+            def _():
+                xsend(n).start()
+
+            @pl.when(n == nc - 1)
+            def _():
+                xlast(0).start()
+                xlast(1).start()
             osend(n).wait_recv()
             base[n] = base[n] + own
+            for k, at in enumerate(EARLY):
+                @pl.when(n == at)
+                def _():
+                    service(k)
             return 0
 
         lax.fori_loop(1, nc, step, 0)
         for n in (nc - 2, nc - 1):
             rsend(n).wait_send()
             osend(n).wait_send()
-
-    def xsend(n):
-        return pltpu.make_async_remote_copy(send.at[n], xrecv.at[n], s_x.at[n], r_x.at[n],
-                                            device_id=xdev, device_id_type=MESH)
 
     pl.run_scoped(produce,
                   pltpu.VMEM((4, 3 * ln, ns), BF16),
@@ -164,7 +210,7 @@
                   pltpu.VMEM((2, 2, ln, CH), F32),
                   pltpu.VMEM((ln, d), BF16))
 
-    def main(acc, wbuf, ystage, abuf0, abuf1):
+    def main(acc, wbuf, abuf0, abuf1):
         def wcopy(n, i):
             src = hbms[i // wj].at[pl.ds(pl.multiple_of(n * CH, CH), CH), pl.ds((i % wj) * WN, WN)]
             return pltpu.make_async_copy(src, wbuf.at[i % NS], s_w.at[i % NS])
@@ -174,51 +220,50 @@
             src = wo_hbm.at[pl.ds(pl.multiple_of(g * CH, CH), CH), pl.ds(i * WN, wd)]
             return pltpu.make_async_copy(src, wbuf.at[i, :, 0:wd], s_w.at[i])
 
-        def ysend(n):
-            return pltpu.make_async_remote_copy(ystage.at[lax.rem(n, 2)], yin.at[n], s_y.at[lax.rem(n, 2)], r_y.at[n],
-                                                device_id=ydev, device_id_type=MESH)
-
         for i in range(NS):
             wcopy(0, i).start()
 
-        def zero(i, _):
-            acc[i] = jnp.zeros(acc.shape[1:], F32)
-            return 0
-        lax.fori_loop(0, acc.shape[0], zero, 0)
         ssq[...] = jnp.zeros_like(ssq)
-
-        def service(n):
-            @pl.when(n >= 2)
-            def _():
-                ysend(n - 2).wait_send()
-            xsend(n).wait_recv()
-            ystage[lax.rem(n, 2)] = (base[n] + xrecv[n]).astype(BF16)
-            ysend(n).start()
 
         def clear(n):
             xsend(n).wait_send()
             send[n] = jnp.zeros(send.shape[1:], F32)
 
-        service(0)
         nj = 3 * wj
 
-        def chunk(n, _):
-            @pl.when(n + 1 < nc)
+        def chunk(n, first):
+            @pl.when((n + 1 >= len(EARLY)) & (n + 1 < nc - 1))
             def _():
                 service(n + 1)
+
+            @pl.when(n == nc - 2)
+            def _():
+                service_last(0)
             @pl.when(n >= 2)
             def _():
                 clear(n - 2)
-            ysend(n).wait_recv()
+            @pl.when(n < nc - 1)
+            def _():
+                ysend(n).wait_recv()
+
+            @pl.when(n == nc - 1)
+            def _():
+                ylast(0).wait_recv()
+                ylast(1).wait_recv()
             yf = yin[n].astype(F32)
             y2 = yf * yf
             ssq[...] += y2[:, 0:128] + y2[:, 128:256] + y2[:, 256:384] + y2[:, 384:512]
             xw = (yf * (nw_ref[n] * SHIFT)).astype(BF16)
             for i in range(nj):
+                if i == LATE:
+                    @pl.when(n == nc - 2)
+                    def _():
+                        service_last(1)
                 wcopy(n, i).wait()
                 for b in range(WN // CH):
                     k = i * (WN // CH) + b
-                    acc[k] += jnp.dot(xw, wbuf[i % NS, :, b * CH:(b + 1) * CH], preferred_element_type=F32)
+                    r = jnp.dot(xw, wbuf[i % NS, :, b * CH:(b + 1) * CH], preferred_element_type=F32)
+                    acc[k] = r if first else acc[k] + r
                 if i + NS < nj:
                     wcopy(n, i + NS).start()
                 else:
@@ -231,13 +276,20 @@
                     @pl.when(n + 1 == nc)
                     def _():
                         ocopy(0, ii).start()
+
+        def later(n, _):
+            chunk(n, False)
             return 0
 
-        lax.fori_loop(0, nc, chunk, 0)
+        chunk(0, True)
+        lax.fori_loop(1, nc, later, 0)
         ysend(nc - 2).wait_send()
-        ysend(nc - 1).wait_send()
-        for n in (nc - 2, nc - 1):
-            clear(n)
+        ylast(0).wait_send()
+        ylast(1).wait_send()
+        clear(nc - 2)
+        xlast(0).wait_send()
+        xlast(1).wait_send()
+        send[nc - 1] = jnp.zeros(send.shape[1:], F32)
         ms = jnp.sum(ssq[...], axis=1, keepdims=True) / d
         rs_ref[...] = jnp.broadcast_to(lax.rsqrt(ms + EPS) * (1.0 / SHIFT), rs_ref.shape)
 
@@ -299,7 +351,6 @@
     pl.run_scoped(main,
                   pltpu.VMEM((3 * ng, ln, CH), F32),
                   pltpu.VMEM((NS, CH, WN), BF16),
-                  pltpu.VMEM((2, ln, CH), BF16),
                   pltpu.VMEM((ln, CH), BF16),
                   pltpu.VMEM((ln, CH), BF16))
 
@@ -332,7 +383,8 @@
                 pltpu.VMEM((nc, ln, CH), BF16),
                 pltpu.VMEM((ln, 128), F32),
                 pltpu.VMEM((ln, 128), F32),
-                sem((2,)), sem((nc,)), sem((2,)), sem((nc,)), sem((nc,)), sem((nc,)), sem((2,)), sem((nc,)),
+                pltpu.VMEM((2, ln, CH), BF16),
+                sem((2,)), sem((nc,)), sem((2,)), sem((nc,)), sem((nc + 1,)), sem((nc + 1,)), sem((3,)), sem((nc + 1,)),
                 sem((NS,)), sem((2, 4)), sem,
             ],
             compiler_params=pltpu.CompilerParams(collective_id=0, has_side_effects=True, vmem_limit_bytes=63000000),

time: 242 us -> 237 us (0.979)
  Pallas kernels: 240 us -> 235 us
    pallas_call x1, Pallas kernels: 240 us -> 235 us  [body(): pl.pallas_call(functools.partial(kernel, n, el, capd), out_shape=pltpu.VM...]
where the time goes in v3:
time: 237 us
  Pallas kernels  235 us (99%)
    pallas_call x1, Pallas kernels, body(): pl.pallas_call(functools.partial(kernel, n, el, capd), out_shape=pltpu.VM...  235 us

profile of v3, /device:TPU:0, one launch (start us, length us, event | category | flops | bytes accessed | tf_op | source)
XLA Modules:
  0.0 236.5 jit_solution(17272162758777419851)
XLA Ops:
  0.0 234.7 %shard_map.100 = bf16[256,7168]{1,0:T(8,128)(2,1)S(1)} custom-call(s32[4,8,256]{2,1,0:T(8,128)} %bitcast.20, s32[4,8,256]{2,1,0:T(8,128)} %bitcast.21, f32[4,8,256]{2,1,0:T(8,128)} %bitcast.22, f32[14,1,512]{2,1,0:T(1,128)} %bitcast.23, bf16[96,4,8,7168]{3,2,1,0:T(8,128)(2,1)} %bitcast.18, bf16[256,7168]{1,0:T(8,128)(2,1)} %bitcast.19, ...), custom_call_target="tpu_custom_call" | custom-call | tf_op jit(solution)/shard_map/pallas_call | solution.py:374
  234.7 1.8 copy.12
